TPU v7x, 32 devices: a whole 2x2x4 slice. The times are simulated.
32 devices in a mesh: dp: 16 (over z, x, core), mp: 2 (over y).
Axes of the slice: x: 2, y: 2, z: 4, core: 2. Of those that a mesh axis runs over, the one named last changes fastest.
Arguments:
- tokens: bfloat16 [2560, 1024], P('dp', 'mp'), may hold values from -6 to 6
- slot_embed: bfloat16 [2560, 1024], P('dp', 'mp'), may hold values from -0.1875 to 0.1875
- price_units: int32 [2560], P('dp'), may hold values from 0 to 1535
- unassigned: int32 [2560], P('dp'), may hold values from 0 to 1, as said below
Outputs:
- new_prices: float32 [2560], P(('dp', 'mp'))
- margins: float32 [2560], P('dp')
- unassigned_count: int32 [], replicated
Inputs may be any that keep to these rules, and one draw needn't show every extreme that they name: At most 128 of the 160 tokens of each index of dp are unassigned, and some index of dp has exactly 128 in every draw.
All inputs are finite; a program needn't handle non-finite values.
Results may differ from a plain program's by a relative error of at most 0.0004.
Values may be sent and summed in bfloat16 or wider, within the bound.
A program may use at most 128 MiB of HBM per device.

v0:
```python
import jax
import jax.numpy as jnp
from jax import lax
from jax.sharding import PartitionSpec as P

BUSY = 128
unit_price = 1.0 / 512.0


def merged(x, axis, combine):
    everything = jax.tree.map(lambda part: lax.all_gather(part, axis), x)
    first = jax.tree.map(lambda part: part[0], everything)

    def turn(k, so_far):
        return combine(so_far, jax.tree.map(lambda part: part[k], everything))

    return lax.fori_loop(1, lax.axis_size(axis), turn, first)


def top_two(values):
    best_value = jnp.max(values, axis=1)
    where_best = jnp.argmax(values, axis=1)
    column_ids = lax.broadcasted_iota(jnp.int32, values.shape, 1)
    second_value = jnp.max(jnp.where(column_ids == where_best[:, None], -jnp.inf, values), axis=1)
    return (best_value, second_value)


def keep_two(first, later):
    best_first, second_first = first
    best_later, second_later = later
    best_value = jnp.maximum(best_first, best_later)
    second_value = jnp.maximum(
        jnp.minimum(best_first, best_later), jnp.maximum(second_first, second_later)
    )
    return (best_value, second_value)


def compact(mask, busy):
    length = mask.shape[0]
    positions = lax.broadcasted_iota(jnp.int32, (length,), 0)
    ordering = jnp.argsort(jnp.where(mask > 0, positions, positions + length))[:busy]
    return (ordering, mask[ordering] > 0)


def spread_back(ordering, is_valid, margin_rows, length):
    positions = lax.broadcasted_iota(jnp.int32, (ordering.shape[0], length), 1)
    hits = (positions == ordering[:, None]) & is_valid[:, None]
    return jnp.sum(jnp.where(hits, margin_rows[:, None], jnp.float32(0.0)), axis=0)


def excess_of(values, second_value, is_valid):
    excess = jnp.where(is_valid[:, None], values - second_value[:, None], -jnp.inf)
    return jnp.max(excess, axis=0)


def on_device(tokens, slot_embed, price_units, unassigned):
    dp_count = lax.axis_size("dp")
    mp_count = lax.axis_size("mp")
    mp_index = lax.axis_index("mp")
    slot_dev = slot_embed.shape[0]
    half = slot_dev // mp_count
    columns = dp_count * half
    ordering, is_valid = compact(unassigned, BUSY)
    bidders = tokens[ordering]
    own_units = lax.dynamic_slice_in_dim(price_units, mp_index * half, half)
    own_prices = own_units.astype(jnp.float32) * unit_price
    whole_bidders = lax.all_gather(bidders, "mp", axis=1, tiled=True)
    slot_rows_whole = lax.all_to_all(slot_embed, "mp", split_axis=0, concat_axis=1, tiled=True)
    unit_all = jnp.zeros((columns,), jnp.int32)
    slot_rows = lax.all_gather(slot_rows_whole, "dp", axis=0, tiled=True)
    unit_rows = lax.all_gather(own_units, "dp", axis=0, tiled=True)
    block = jnp.einsum("bd,sd->bs", whole_bidders, slot_rows, preferred_element_type=jnp.float32)
    unit_all = lax.dynamic_update_slice_in_dim(unit_all, unit_rows, jnp.int32(0), 0)
    scores, unit_all = (block, unit_all)
    values = scores - (unit_all.astype(jnp.float32) * unit_price)[None, :]
    best_value, second_value = merged(top_two(values), "mp", keep_two)
    terms = excess_of(values, second_value, is_valid).reshape(dp_count, half)
    owner_terms = lax.all_to_all(terms, "dp", split_axis=0, concat_axis=0, tiled=True)
    highest = jnp.max(owner_terms, axis=0)
    new_prices = own_prices + jnp.maximum(highest, jnp.float32(0.0))
    margin_rows = jnp.where(is_valid, best_value - second_value, jnp.float32(0.0))
    margins = spread_back(ordering, is_valid, margin_rows, unassigned.shape[0])
    bidder_total = lax.psum(jnp.sum(unassigned), "dp")
    return (new_prices, margins, bidder_total)


def solution(mesh):
    return jax.shard_map(
        on_device,
        mesh=mesh,
        in_specs=(P("dp", "mp"), P("dp", "mp"), P("dp"), P("dp")),
        out_specs=(P(("dp", "mp")), P("dp"), P()),
        check_vma=False,
    )
```

profile of v0, /device:TPU:0, one launch (start us, length us, event | category | flops | bytes accessed | tf_op | source)
XLA Modules:
  0.0 91.2 jit_solution(4303682870376259929)
XLA Ops:
  7.2 0.0 copy-start
  7.2 0.0 all-gather.7.cloned.1.call-start
  7.2 9.2 %all_to_all.28 = bf16[2,80,512]{2,1,0:T(8,128)(2,1)S(1)} all-to-all(bf16[2,80,512]{2,1,0:T(8,128)(2,1)} %bitcast.19), channel_id=1, replica_groups=mesh['dp'=16,'mp'=2] {'mp'}, dimensions={0} | all-to-all | bytes 327680 | tf_op jit(solution)/shard_map/all_to_all | solution.py:68
  16.4 0.7 copy.12
  17.1 0.0 all-gather.7.cloned.1.call-update
  17.1 1.3 %fusion.6 = (s32[]{:T(128)}, s32[160]{0:T(256)S(1)}) fusion(s32[160]{0:T(256)} %param.7), kind=kLoop, calls=%fused_computation.23 | loop fusion | flops 639 | bytes 1284 | tf_op jit(solution)/shard_map/reduce_sum | solution.py:83
  18.4 3.2 %sort.17 = (s32[160]{0:T(256)}, s32[160]{0:T(256)S(1)}) sort(s32[160]{0:T(256)S(1)} %get-tuple-element.35, s32[160]{0:T(256)S(1)} %iota.27), dimensions={0}, to_apply=%region_0.1 | sort | flops 1280 | bytes 2560 | tf_op jit(solution)/shard_map/jit(argsort)/sort | solution.py:41
  21.6 1.6 %gather_fusion = s32[128]{0:T(128)S(1)} fusion(s32[160]{0:T(256)} %param.7, s32[1024]{0:T(1024)S(1)} %pad_clamp_fusion), kind=kCustom, calls=%fused_computation | custom fusion | bytes 1536 | tf_op jit(solution)/shard_map/gather | solution.py:42
  23.3 0.0 copy-done
  23.3 0.8 gather_fusion.1
  24.1 1.2 %dynamic-slice = u32[1]{0:T(128)} dynamic-slice(u32[32]{0:T(128)} %constant.16, u32[]{:T(128)S(6)} %add.30), dynamic_slice_sizes={1} | dynamic-slice | bytes 12
  26.0 0.9 dynamic-slice_dynamic-update-slice_fusion
  26.9 13.7 %all-reduce.1 = (s32[1280]{0:T(1024)S(1)}, s32[]{:T(128)}) all-reduce(s32[1280]{0:T(1024)S(1)} %dynamic-slice_dynamic-update-slice_fusion, s32[]{:T(128)} %get-tuple-element.34), channel_id=1, replica_groups=mesh['dp'=16,'mp'=2] {'dp'}, use_global_device_ids=true, to_apply=%add | all-reduce | flops 1281 | bytes 10248
  40.6 5.6 %all-gather = bf16[128,1024]{1,0:T(8,128)(2,1)S(1)} all-gather(bf16[128,512]{1,0:T(8,128)(2,1)S(1)} %gather_fusion.1), channel_id=2, replica_groups=mesh['dp'=16,'mp'=2] {'mp'}, dimensions={1}, use_global_device_ids=true | all-gather | bytes 393216 | tf_op jit(solution)/shard_map/all_gather | solution.py:67
  46.2 0.0 copy-start.1
  46.3 14.8 %all-gather.7.cloned.1.call-done = bf16[1280,1024]{1,0:T(8,128)(2,1)} async-done(((bf16[80,1024]{1,0:T(8,128)(2,1)}), bf16[1280,1024]{1,0:T(8,128)(2,1)}) %all-gather.7.cloned.1.call-update) | async-done | bytes 2621456 | tf_op jit(solution)/shard_map/all_gather | solution.py:70
  61.0 2.7 %convolution_subtract_fusion = f32[128,1280]{1,0:T(8,128)S(1)} fusion(bf16[128,1024]{1,0:T(8,128)(2,1)S(1)} %all-gather, bf16[1280,1024]{1,0:T(8,128)(2,1)} %all-gather.7.cloned.1.call-done, f32[1280]{0:T(1024)S(1)} %convert_multiply_fusion), kind=kOutput, calls=%fused_computation.2 | convolution fusion | flops 335708160 | bytes 3544064 | tf_op jit(solution)/shard_map/bd,sd->bs/dot_general | solution.py:72
  63.8 0.4 iota_reduce_fusion
  64.2 4.2 %all-gather.3 = f32[2,1,128]{2,1,0:T(1,128)S(1)} all-gather(f32[1,1,128]{2,1,0:T(1,128)S(1)} %bitcast.21), channel_id=3, replica_groups=mesh['dp'=16,'mp'=2] {'mp'}, dimensions={0}, use_global_device_ids=true | all-gather | bytes 1536 | tf_op jit(solution)/shard_map/all_gather | solution.py:11
  68.4 0.2 select_reduce_fusion.1
  68.6 4.2 %all-gather.4 = f32[2,1,128]{2,1,0:T(1,128)S(1)} all-gather(f32[1,1,128]{2,1,0:T(1,128)S(1)} %bitcast.22), channel_id=4, replica_groups=mesh['dp'=16,'mp'=2] {'mp'}, dimensions={0}, use_global_device_ids=true | all-gather | bytes 1536 | tf_op jit(solution)/shard_map/all_gather | solution.py:11
  72.9 0.1 select_reduce_fusion
  73.0 0.7 all_to_all.24
  73.7 3.6 %all-to-all-start.1 = ((f32[16,1,80]{2,1,0:T(1,128)}), f32[16,1,80]{2,1,0:T(1,128)S(1)}, u32[]{:S(2)}, u32[]{:S(2)}) async-start(f32[16,1,80]{2,1,0:T(1,128)} %all_to_all.24), calls=%async_computation.1 | async-start | bytes 16384 | tf_op jit(solution)/shard_map/all_to_all | solution.py:78
  77.3 0.7 select_reduce_fusion.2
  77.9 5.8 %all-to-all-done.1 = f32[16,1,80]{2,1,0:T(1,128)S(1)} async-done(((f32[16,1,80]{2,1,0:T(1,128)}), f32[16,1,80]{2,1,0:T(1,128)S(1)}, u32[]{:S(2)}, u32[]{:S(2)}) %all-to-all-start.1) | async-done | bytes 5152 | tf_op jit(solution)/shard_map/all_to_all | solution.py:78
  83.7 0.0 copy-done.1
  83.7 0.6 maximum_add_fusion
  (8 shorter events, 0.1 us)
Async XLA Ops:
  7.2 16.1 %copy-start = (bf16[160,512]{1,0:T(8,128)(2,1)S(1)}, bf16[160,512]{1,0:T(8,128)(2,1)}, u32[]{:S(2)}) copy-start(bf16[160,512]{1,0:T(8,128)(2,1)} %param.4) | copy-start | bytes 491524
  7.2 53.9 %all-gather.7.cloned.1.call-start = ((), (), s32[]{:S(2)}) async-start(), calls=%async_computation.2 | async-start | bytes 2785280 | tf_op jit(solution)/shard_map/all_gather | solution.py:70
  46.2 37.5 %copy-start.1 = (s32[160]{0:T(256)S(1)}, s32[160]{0:T(256)}, u32[]{:S(2)}) copy-start(s32[160]{0:T(256)} %param.6) | copy-start | bytes 1924
  73.7 10.0 %all-to-all-start.1 = ((f32[16,1,80]{2,1,0:T(1,128)}), f32[16,1,80]{2,1,0:T(1,128)S(1)}, u32[]{:S(2)}, u32[]{:S(2)}) async-start(f32[16,1,80]{2,1,0:T(1,128)} %all_to_all.24), calls=%async_computation.1 | async-start | bytes 16384 | tf_op jit(solution)/shard_map/all_to_all | solution.py:78
Sparse Core Ops, SparseCore 0:
  17.2 43.7 all-gather.6
where the time goes:
time: 91.5 us; the launch traced here: 91.2 us
  blocking collectives  37 us (40%)
  waiting for transfers between devices  20.6 us (23%)
  between operations  14.7 us (16%)
  other arithmetic  6.56 us (7%)
  local copies, waits for them, and re-layouts  5.97 us (7%)
  starting transfers between devices  3.59 us (4%)
  matrix products  2.73 us (3%)
    all_gather x1, waiting for transfers between devices, on_device(): slot_rows = lax.all_gather(slot_rows_whole, 'dp', axis=0, tiled=True)  14.8 us
    unnamed x1, blocking collectives  13.7 us
    all_to_all x1, blocking collectives, on_device(): lax.all_to_all(slot_embed, 'mp', split_axis=0, concat_axis=1, tiled=True)  9.2 us
    all_gather x2, blocking collectives, merged(): everything = jax.tree.map(lambda part: lax.all_gather(part, axis), x)  8.47 us
    all_to_all x1, waiting for transfers between devices, on_device(): lax.all_to_all(terms, 'dp', split_axis=0, concat_axis=0, tiled=True)  5.75 us
    all_gather x1, blocking collectives, on_device(): whole_bidders = lax.all_gather(bidders, 'mp', axis=1, tiled=True)  5.62 us
    all_to_all x1, starting transfers between devices, on_device(): lax.all_to_all(terms, 'dp', split_axis=0, concat_axis=0, tiled=True)  3.55 us
    sort x1, other arithmetic, compact(): jnp.argsort(jnp.where(mask > 0, positions, positions + length))[:busy]  3.17 us
  transfers between devices with their start and end apart: 2, of which 2 were waited for; matrix products, arithmetic and copies ran while one was open for 11% of the time, Pallas kernels for 0%

commit v1 on v0

--- a/solution.py
+++ b/solution.py
@@ -5,6 +5,20 @@
 
 BUSY = 128
 unit_price = 1.0 / 512.0
+
+
+def ring_apply(shard, axis, dim, make, out_dim):
+    ways, here, turn = (lax.axis_size(axis), lax.axis_index(axis), shard.shape[dim])
+    earlier, later = ([], [])
+    going_up = going_down = shard
+    for far in range(ways // 2 + 1):
+        earlier.append(make(going_up, (here - far) % ways * turn))
+        if 0 < far < ways - ways // 2:
+            later.append(make(going_down, (here + far) % ways * turn))
+        going_up = lax.ppermute(going_up, axis, [(d, (d + 1) % ways) for d in range(ways)])
+        going_down = lax.ppermute(going_down, axis, [(d, (d - 1) % ways) for d in range(ways)])
+    line = jnp.concatenate([*earlier[::-1], *later], axis=out_dim)
+    return jnp.roll(line, (here - ways // 2) * earlier[0].shape[out_dim], axis=out_dim)
 
 
 def merged(x, axis, combine):
@@ -67,9 +81,16 @@
     whole_bidders = lax.all_gather(bidders, "mp", axis=1, tiled=True)
     slot_rows_whole = lax.all_to_all(slot_embed, "mp", split_axis=0, concat_axis=1, tiled=True)
     unit_all = jnp.zeros((columns,), jnp.int32)
-    slot_rows = lax.all_gather(slot_rows_whole, "dp", axis=0, tiled=True)
     unit_rows = lax.all_gather(own_units, "dp", axis=0, tiled=True)
-    block = jnp.einsum("bd,sd->bs", whole_bidders, slot_rows, preferred_element_type=jnp.float32)
+    block = ring_apply(
+        slot_rows_whole,
+        "dp",
+        0,
+        lambda shard, offset: jnp.einsum(
+            "bd,sd->bs", whole_bidders, shard, preferred_element_type=jnp.float32
+        ),
+        1,
+    )
     unit_all = lax.dynamic_update_slice_in_dim(unit_all, unit_rows, jnp.int32(0), 0)
     scores, unit_all = (block, unit_all)
     values = scores - (unit_all.astype(jnp.float32) * unit_price)[None, :]

time: 91.5 us -> 108 us (1.18)
  starting transfers between devices: 3.59 us -> 31.1 us
  between operations: 14.7 us -> 1.71 us
  waiting for transfers between devices: 20.6 us -> 24.5 us
  local copies, waits for them, and re-layouts: 5.97 us -> 4.07 us
    ppermute x0 -> x15, starting transfers between devices: none -> 27.7 us  [the longest x7 27.1 us: ring_apply(): lax.ppermute(going_down, axis, [(d, (d - 1) % ways) for d in range(ways)])]
    ppermute x0 -> x15, waiting for transfers between devices: none -> 18.8 us  [the longest x8 13.8 us: ring_apply(): lax.ppermute(going_up, axis, [(d, (d + 1) % ways) for d in range(ways)])]
    all_gather x1 -> x0, waiting for transfers between devices: 14.8 us -> none  [on_device(): slot_rows = lax.all_gather(slot_rows_whole, 'dp', axis=0, tiled=True)]
    unnamed x7 -> x24, local copies, waits for them, and re-layouts: 2.14 us -> 0.89 us
    dot_general x1 -> x16, matrix products: 2.73 us -> 3.4 us  [on_device(): jnp.einsum('bd,sd->bs', whole_bidders, shard, preferred_element_type=jnp....]
  transfers between devices with their start and end apart: 2 -> 16, of which waited for: 2 -> 8; matrix products, arithmetic and copies ran while one was open for 11% -> 11% of each run, Pallas kernels for 0% -> 0%
where the time goes in v1:
time: 108 us
  blocking collectives  36.3 us (34%)
  starting transfers between devices  31.1 us (29%)
  waiting for transfers between devices  24.5 us (23%)
  other arithmetic  6.93 us (6%)
  local copies, waits for them, and re-layouts  4.07 us (4%)
  matrix products  3.4 us (3%)
  between operations  1.71 us (2%)
    ppermute x7, starting transfers between devices, ring_apply(): lax.ppermute(going_down, axis, [(d, (d - 1) % ways) for d in range(ways)])  27.1 us
    ppermute x8, waiting for transfers between devices, ring_apply(): lax.ppermute(going_up, axis, [(d, (d + 1) % ways) for d in range(ways)])  13.8 us
    unnamed x1, blocking collectives  13 us
    all_to_all x1, blocking collectives, on_device(): lax.all_to_all(slot_embed, 'mp', split_axis=0, concat_axis=1, tiled=True)  9.2 us
    all_gather x2, blocking collectives, merged(): everything = jax.tree.map(lambda part: lax.all_gather(part, axis), x)  8.46 us
    all_to_all x1, waiting for transfers between devices, on_device(): lax.all_to_all(terms, 'dp', split_axis=0, concat_axis=0, tiled=True)  5.71 us
    all_gather x1, blocking collectives, on_device(): whole_bidders = lax.all_gather(bidders, 'mp', axis=1, tiled=True)  5.62 us
    ppermute x7, waiting for transfers between devices, ring_apply(): lax.ppermute(going_down, axis, [(d, (d - 1) % ways) for d in range(ways)])  5 us
  transfers between devices with their start and end apart: 16, of which 8 were waited for; matrix products, arithmetic and copies ran while one was open for 11% of the time, Pallas kernels for 0%

profile of v1, /device:TPU:0, one launch (start us, length us, event | category | flops | bytes accessed | tf_op | source)
XLA Modules:
  0.0 108.0 jit_solution(499295315003744248)
XLA Ops:
  0.7 9.2 %all_to_all.28 = bf16[2,80,512]{2,1,0:T(8,128)(2,1)S(1)} all-to-all(bf16[2,80,512]{2,1,0:T(8,128)(2,1)} %bitcast.51), channel_id=1, replica_groups=mesh['dp'=16,'mp'=2] {'mp'}, dimensions={0} | all-to-all | bytes 327680 | tf_op jit(solution)/shard_map/all_to_all | solution.py:82
  10.0 7.4 %collective-permute-done = bf16[80,1024]{1,0:T(8,128)(2,1)S(1)} collective-permute-done((bf16[80,1024]{1,0:T(8,128)(2,1)S(1)}, bf16[80,1024]{1,0:T(8,128)(2,1)S(1)}, u32[]{:S(2)}, u32[]{:S(2)}) %collective-permute-start) | collective-permute-done | bytes 163872 | tf_op jit(solution)/shard_map/ppermute | solution.py:18
  17.4 4.4 %collective-permute-start.8 = (bf16[80,1024]{1,0:T(8,128)(2,1)S(1)}, bf16[80,1024]{1,0:T(8,128)(2,1)S(1)}, u32[]{:S(2)}, u32[]{:S(2)}) collective-permute-start(bf16[80,1024]{1,0:T(8,128)(2,1)S(1)} %bitcast.48), channel_id=1, source_target_pairs={{0,30},{2,0},{4,2},{6,4},{8,6},{10,8},{12,10},{14,12},{16,14},{18,... | collective-permute-start | bytes 491528 | tf_op jit(solution)/shard_map/ppermute | solution.py:19
  21.8 3.0 %collective-permute-done.1 = bf16[80,1024]{1,0:T(8,128)(2,1)S(1)} collective-permute-done((bf16[80,1024]{1,0:T(8,128)(2,1)S(1)}, bf16[80,1024]{1,0:T(8,128)(2,1)S(1)}, u32[]{:S(2)}, u32[]{:S(2)}) %collective-permute-start.1) | collective-permute-done | bytes 163872 | tf_op jit(solution)/shard_map/ppermute | solution.py:18
  24.8 4.5 %collective-permute-start.9 = (bf16[80,1024]{1,0:T(8,128)(2,1)S(1)}, bf16[80,1024]{1,0:T(8,128)(2,1)S(1)}, u32[]{:S(2)}, u32[]{:S(2)}) collective-permute-start(bf16[80,1024]{1,0:T(8,128)(2,1)S(1)} %collective-permute-done.8), channel_id=1, source_target_pairs={{0,30},{2,0},{4,2},{6,4},{8,6},{10,8},{12,10},{14,12},{16,14},{18,... | collective-permute-start | bytes 491528 | tf_op jit(solution)/shard_map/ppermute | solution.py:19
  29.4 2.9 %collective-permute-done.2 = bf16[80,1024]{1,0:T(8,128)(2,1)S(1)} collective-permute-done((bf16[80,1024]{1,0:T(8,128)(2,1)S(1)}, bf16[80,1024]{1,0:T(8,128)(2,1)S(1)}, u32[]{:S(2)}, u32[]{:S(2)}) %collective-permute-start.2) | collective-permute-done | bytes 163872 | tf_op jit(solution)/shard_map/ppermute | solution.py:18
  32.3 1.3 %fusion.6 = (s32[]{:T(128)}, s32[160]{0:T(256)S(1)}) fusion(s32[160]{0:T(256)} %param.7), kind=kLoop, calls=%fused_computation.55 | loop fusion | flops 639 | bytes 1284 | tf_op jit(solution)/shard_map/reduce_sum | solution.py:104
  33.6 3.2 %sort.17 = (s32[160]{0:T(256)}, s32[160]{0:T(256)S(1)}) sort(s32[160]{0:T(256)S(1)} %get-tuple-element.35, s32[160]{0:T(256)S(1)} %iota.27), dimensions={0}, to_apply=%region_0.1 | sort | flops 1280 | bytes 2560 | tf_op jit(solution)/shard_map/jit(argsort)/sort | solution.py:55
  36.8 4.4 %collective-permute-start.10 = (bf16[80,1024]{1,0:T(8,128)(2,1)S(1)}, bf16[80,1024]{1,0:T(8,128)(2,1)S(1)}, u32[]{:S(2)}, u32[]{:S(2)}) collective-permute-start(bf16[80,1024]{1,0:T(8,128)(2,1)S(1)} %collective-permute-done.9), channel_id=1, source_target_pairs={{0,30},{2,0},{4,2},{6,4},{8,6},{10,8},{12,10},{14,12},{16,14},{18,... | collective-permute-start | bytes 491528 | tf_op jit(solution)/shard_map/ppermute | solution.py:19
  41.3 1.6 %gather_fusion = s32[128]{0:T(128)S(1)} fusion(s32[160]{0:T(256)} %param.7, s32[1024]{0:T(1024)S(1)} %pad_clamp_fusion), kind=kCustom, calls=%fused_computation | custom fusion | bytes 1536 | tf_op jit(solution)/shard_map/gather | solution.py:56
  42.9 0.8 gather_fusion.1
  43.8 0.6 dynamic-slice
  45.0 4.5 %collective-permute-start.11 = (bf16[80,1024]{1,0:T(8,128)(2,1)S(1)}, bf16[80,1024]{1,0:T(8,128)(2,1)S(1)}, u32[]{:S(2)}, u32[]{:S(2)}) collective-permute-start(bf16[80,1024]{1,0:T(8,128)(2,1)S(1)} %collective-permute-done.10), channel_id=1, source_target_pairs={{0,30},{2,0},{4,2},{6,4},{8,6},{10,8},{12,10},{14,12},{16,14},{18,... | collective-permute-start | bytes 491528 | tf_op jit(solution)/shard_map/ppermute | solution.py:19
  49.5 0.2 dynamic-slice_dynamic-update-slice_fusion
  49.7 13.0 %all-reduce.1 = (s32[1280]{0:T(1024)S(1)}, s32[]{:T(128)}) all-reduce(s32[1280]{0:T(1024)S(1)} %dynamic-slice_dynamic-update-slice_fusion, s32[]{:T(128)} %get-tuple-element.34), channel_id=1, replica_groups=mesh['dp'=16,'mp'=2] {'dp'}, use_global_device_ids=true, to_apply=%add | all-reduce | flops 1281 | bytes 10248
  62.7 5.6 %all-gather = bf16[128,1024]{1,0:T(8,128)(2,1)S(1)} all-gather(bf16[128,512]{1,0:T(8,128)(2,1)S(1)} %gather_fusion.1), channel_id=2, replica_groups=mesh['dp'=16,'mp'=2] {'mp'}, dimensions={1}, use_global_device_ids=true | all-gather | bytes 393216 | tf_op jit(solution)/shard_map/all_gather | solution.py:81
  68.4 0.5 collective-permute-start.6
  68.9 2.3 %collective-permute-done.12 = bf16[80,1024]{1,0:T(8,128)(2,1)S(1)} collective-permute-done((bf16[80,1024]{1,0:T(8,128)(2,1)S(1)}, bf16[80,1024]{1,0:T(8,128)(2,1)S(1)}, u32[]{:S(2)}, u32[]{:S(2)}) %collective-permute-start.12) | collective-permute-done | bytes 163872 | tf_op jit(solution)/shard_map/ppermute | solution.py:19
  71.2 4.6 %collective-permute-start.13 = (bf16[80,1024]{1,0:T(8,128)(2,1)S(1)}, bf16[80,1024]{1,0:T(8,128)(2,1)S(1)}, u32[]{:S(2)}, u32[]{:S(2)}) collective-permute-start(bf16[80,1024]{1,0:T(8,128)(2,1)S(1)} %collective-permute-done.12), channel_id=1, source_target_pairs={{0,30},{2,0},{4,2},{6,4},{8,6},{10,8},{12,10},{14,12},{16,14},{18,... | collective-permute-start | bytes 491528 | tf_op jit(solution)/shard_map/ppermute | solution.py:19
  76.0 2.7 %collective-permute-done.13 = bf16[80,1024]{1,0:T(8,128)(2,1)S(1)} collective-permute-done((bf16[80,1024]{1,0:T(8,128)(2,1)S(1)}, bf16[80,1024]{1,0:T(8,128)(2,1)S(1)}, u32[]{:S(2)}, u32[]{:S(2)}) %collective-permute-start.13) | collective-permute-done | bytes 163872 | tf_op jit(solution)/shard_map/ppermute | solution.py:19
  78.6 4.6 %collective-permute-start.14 = (bf16[80,1024]{1,0:T(8,128)(2,1)S(1)}, bf16[80,1024]{1,0:T(8,128)(2,1)S(1)}, u32[]{:S(2)}, u32[]{:S(2)}) collective-permute-start(bf16[80,1024]{1,0:T(8,128)(2,1)S(1)} %collective-permute-done.13), channel_id=1, source_target_pairs={{0,30},{2,0},{4,2},{6,4},{8,6},{10,8},{12,10},{14,12},{16,14},{18,... | collective-permute-start | bytes 491528 | tf_op jit(solution)/shard_map/ppermute | solution.py:19
  83.2 0.3 collective-permute-done.7
  83.5 0.2 constant_dynamic-update-slice_fusion.31
  83.7 0.2 constant_dynamic-update-slice_fusion.30
  83.9 0.2 constant_dynamic-update-slice_fusion.29
  84.2 0.2 constant_dynamic-update-slice_fusion.28
  84.4 0.2 constant_dynamic-update-slice_fusion.27
  84.6 0.2 constant_dynamic-update-slice_fusion.26
  84.8 0.2 constant_dynamic-update-slice_fusion.25
  85.0 0.2 constant_dynamic-update-slice_fusion.24
  85.3 0.2 constant_dynamic-update-slice_fusion.23
  85.5 0.2 constant_dynamic-update-slice_fusion.22
  85.7 0.2 constant_dynamic-update-slice_fusion.21
  85.9 0.2 constant_dynamic-update-slice_fusion.20
  86.2 0.2 constant_dynamic-update-slice_fusion.19
  86.4 0.2 constant_dynamic-update-slice_fusion.18
  86.6 0.2 constant_dynamic-update-slice_fusion.17
  86.8 0.2 constant_dynamic-update-slice_fusion.16
  87.3 0.4 iota_reduce_fusion
  87.7 0.3 select_reduce_fusion.1
  88.0 4.2 %all-gather.4 = f32[2,1,128]{2,1,0:T(1,128)S(1)} all-gather(f32[1,1,128]{2,1,0:T(1,128)S(1)} %bitcast.54), channel_id=4, replica_groups=mesh['dp'=16,'mp'=2] {'mp'}, dimensions={0}, use_global_device_ids=true | all-gather | bytes 1536 | tf_op jit(solution)/shard_map/all_gather | solution.py:25
  92.2 4.2 %all-gather.3 = f32[2,1,128]{2,1,0:T(1,128)S(1)} all-gather(f32[1,1,128]{2,1,0:T(1,128)S(1)} %bitcast.53), channel_id=3, replica_groups=mesh['dp'=16,'mp'=2] {'mp'}, dimensions={0}, use_global_device_ids=true | all-gather | bytes 1536 | tf_op jit(solution)/shard_map/all_gather | solution.py:25
  96.4 0.4 select_reduce_fusion
  96.9 0.7 all_to_all.24
  97.5 3.4 %all-to-all-start.1 = ((f32[16,1,80]{2,1,0:T(1,128)}), f32[16,1,80]{2,1,0:T(1,128)S(1)}, u32[]{:S(2)}, u32[]{:S(2)}) async-start(f32[16,1,80]{2,1,0:T(1,128)} %all_to_all.24), calls=%async_computation.1 | async-start | bytes 16384 | tf_op jit(solution)/shard_map/all_to_all | solution.py:99
  101.0 0.7 select_reduce_fusion.2
  101.7 5.7 %all-to-all-done.1 = f32[16,1,80]{2,1,0:T(1,128)S(1)} async-done(((f32[16,1,80]{2,1,0:T(1,128)}), f32[16,1,80]{2,1,0:T(1,128)S(1)}, u32[]{:S(2)}, u32[]{:S(2)}) %all-to-all-start.1) | async-done | bytes 5152 | tf_op jit(solution)/shard_map/all_to_all | solution.py:99
  107.4 0.6 maximum_add_fusion
  (48 shorter events, 0.4 us)
Async XLA Ops:
  0.6 42.3 %copy-start = (bf16[160,512]{1,0:T(8,128)(2,1)S(1)}, bf16[160,512]{1,0:T(8,128)(2,1)}, u32[]{:S(2)}) copy-start(bf16[160,512]{1,0:T(8,128)(2,1)} %param.4) | copy-start | bytes 491524
  0.6 43.1 %copy-start.2 = (u32[32]{0:T(128)S(1)}, u32[32]{0:T(128)}, u32[]{:S(2)}) copy-start(u32[32]{0:T(128)} %constant.62) | copy-start | bytes 388
  0.7 48.9 %copy-start.1 = (s32[160]{0:T(256)S(1)}, s32[160]{0:T(256)}, u32[]{:S(2)}) copy-start(s32[160]{0:T(256)} %param.6) | copy-start | bytes 1924
  9.9 7.5 %collective-permute-start = (bf16[80,1024]{1,0:T(8,128)(2,1)S(1)}, bf16[80,1024]{1,0:T(8,128)(2,1)S(1)}, u32[]{:S(2)}, u32[]{:S(2)}) collective-permute-start(bf16[80,1024]{1,0:T(8,128)(2,1)S(1)} %bitcast.47), channel_id=1, source_target_pairs={{0,2},{2,4},{4,6},{6,8},{8,10},{10,12},{12,14},{14,16},{16,18},{18... | collective-permute-start | bytes 491528 | tf_op jit(solution)/shard_map/ppermute | solution.py:18
  17.4 7.5 %collective-permute-start.1 = (bf16[80,1024]{1,0:T(8,128)(2,1)S(1)}, bf16[80,1024]{1,0:T(8,128)(2,1)S(1)}, u32[]{:S(2)}, u32[]{:S(2)}) collective-permute-start(bf16[80,1024]{1,0:T(8,128)(2,1)S(1)} %collective-permute-done), channel_id=1, source_target_pairs={{0,2},{2,4},{4,6},{6,8},{8,10},{10,12},{12,14},{14,16},{16,18},{18... | collective-permute-start | bytes 491528 | tf_op jit(solution)/shard_map/ppermute | solution.py:18
  17.4 7.5 %collective-permute-start.8 = (bf16[80,1024]{1,0:T(8,128)(2,1)S(1)}, bf16[80,1024]{1,0:T(8,128)(2,1)S(1)}, u32[]{:S(2)}, u32[]{:S(2)}) collective-permute-start(bf16[80,1024]{1,0:T(8,128)(2,1)S(1)} %bitcast.48), channel_id=1, source_target_pairs={{0,30},{2,0},{4,2},{6,4},{8,6},{10,8},{12,10},{14,12},{16,14},{18,... | collective-permute-start | bytes 491528 | tf_op jit(solution)/shard_map/ppermute | solution.py:19
  24.8 7.4 %collective-permute-start.2 = (bf16[80,1024]{1,0:T(8,128)(2,1)S(1)}, bf16[80,1024]{1,0:T(8,128)(2,1)S(1)}, u32[]{:S(2)}, u32[]{:S(2)}) collective-permute-start(bf16[80,1024]{1,0:T(8,128)(2,1)S(1)} %collective-permute-done.1), channel_id=1, source_target_pairs={{0,2},{2,4},{4,6},{6,8},{8,10},{10,12},{12,14},{14,16},{16,18},{18... | collective-permute-start | bytes 491528 | tf_op jit(solution)/shard_map/ppermute | solution.py:18
  24.8 11.9 %collective-permute-start.9 = (bf16[80,1024]{1,0:T(8,128)(2,1)S(1)}, bf16[80,1024]{1,0:T(8,128)(2,1)S(1)}, u32[]{:S(2)}, u32[]{:S(2)}) collective-permute-start(bf16[80,1024]{1,0:T(8,128)(2,1)S(1)} %collective-permute-done.8), channel_id=1, source_target_pairs={{0,30},{2,0},{4,2},{6,4},{8,6},{10,8},{12,10},{14,12},{16,14},{18,... | collective-permute-start | bytes 491528 | tf_op jit(solution)/shard_map/ppermute | solution.py:19
  32.3 8.9 %collective-permute-start.3 = (bf16[80,1024]{1,0:T(8,128)(2,1)S(1)}, bf16[80,1024]{1,0:T(8,128)(2,1)S(1)}, u32[]{:S(2)}, u32[]{:S(2)}) collective-permute-start(bf16[80,1024]{1,0:T(8,128)(2,1)S(1)} %collective-permute-done.2), channel_id=1, source_target_pairs={{0,2},{2,4},{4,6},{6,8},{8,10},{10,12},{12,14},{14,16},{16,18},{18... | collective-permute-start | bytes 491528 | tf_op jit(solution)/shard_map/ppermute | solution.py:18
  36.8 8.3 %collective-permute-start.10 = (bf16[80,1024]{1,0:T(8,128)(2,1)S(1)}, bf16[80,1024]{1,0:T(8,128)(2,1)S(1)}, u32[]{:S(2)}, u32[]{:S(2)}) collective-permute-start(bf16[80,1024]{1,0:T(8,128)(2,1)S(1)} %collective-permute-done.9), channel_id=1, source_target_pairs={{0,30},{2,0},{4,2},{6,4},{8,6},{10,8},{12,10},{14,12},{16,14},{18,... | collective-permute-start | bytes 491528 | tf_op jit(solution)/shard_map/ppermute | solution.py:19
  41.2 8.3 %collective-permute-start.4 = (bf16[80,1024]{1,0:T(8,128)(2,1)S(1)}, bf16[80,1024]{1,0:T(8,128)(2,1)S(1)}, u32[]{:S(2)}, u32[]{:S(2)}) collective-permute-start(bf16[80,1024]{1,0:T(8,128)(2,1)S(1)} %collective-permute-done.3), channel_id=1, source_target_pairs={{0,2},{2,4},{4,6},{6,8},{8,10},{10,12},{12,14},{14,16},{16,18},{18... | collective-permute-start | bytes 491528 | tf_op jit(solution)/shard_map/ppermute | solution.py:18
  45.0 23.3 %collective-permute-start.11 = (bf16[80,1024]{1,0:T(8,128)(2,1)S(1)}, bf16[80,1024]{1,0:T(8,128)(2,1)S(1)}, u32[]{:S(2)}, u32[]{:S(2)}) collective-permute-start(bf16[80,1024]{1,0:T(8,128)(2,1)S(1)} %collective-permute-done.10), channel_id=1, source_target_pairs={{0,30},{2,0},{4,2},{6,4},{8,6},{10,8},{12,10},{14,12},{16,14},{18,... | collective-permute-start | bytes 491528 | tf_op jit(solution)/shard_map/ppermute | solution.py:19
  49.5 18.9 %collective-permute-start.5 = (bf16[80,1024]{1,0:T(8,128)(2,1)S(1)}, bf16[80,1024]{1,0:T(8,128)(2,1)S(1)}, u32[]{:S(2)}, u32[]{:S(2)}) collective-permute-start(bf16[80,1024]{1,0:T(8,128)(2,1)S(1)} %collective-permute-done.4), channel_id=1, source_target_pairs={{0,2},{2,4},{4,6},{6,8},{8,10},{10,12},{12,14},{14,16},{16,18},{18... | collective-permute-start | bytes 491528 | tf_op jit(solution)/shard_map/ppermute | solution.py:18
  68.4 2.8 %collective-permute-start.12 = (bf16[80,1024]{1,0:T(8,128)(2,1)S(1)}, bf16[80,1024]{1,0:T(8,128)(2,1)S(1)}, u32[]{:S(2)}, u32[]{:S(2)}) collective-permute-start(bf16[80,1024]{1,0:T(8,128)(2,1)S(1)} %collective-permute-done.11), channel_id=1, source_target_pairs={{0,30},{2,0},{4,2},{6,4},{8,6},{10,8},{12,10},{14,12},{16,14},{18,... | collective-permute-start | bytes 491528 | tf_op jit(solution)/shard_map/ppermute | solution.py:19
  68.4 7.6 %collective-permute-start.6 = (bf16[80,1024]{1,0:T(8,128)(2,1)S(1)}, bf16[80,1024]{1,0:T(8,128)(2,1)S(1)}, u32[]{:S(2)}, u32[]{:S(2)}) collective-permute-start(bf16[80,1024]{1,0:T(8,128)(2,1)S(1)} %collective-permute-done.5), channel_id=1, source_target_pairs={{0,2},{2,4},{4,6},{6,8},{8,10},{10,12},{12,14},{14,16},{16,18},{18... | collective-permute-start | bytes 491528 | tf_op jit(solution)/shard_map/ppermute | solution.py:18
  71.2 7.4 %collective-permute-start.13 = (bf16[80,1024]{1,0:T(8,128)(2,1)S(1)}, bf16[80,1024]{1,0:T(8,128)(2,1)S(1)}, u32[]{:S(2)}, u32[]{:S(2)}) collective-permute-start(bf16[80,1024]{1,0:T(8,128)(2,1)S(1)} %collective-permute-done.12), channel_id=1, source_target_pairs={{0,30},{2,0},{4,2},{6,4},{8,6},{10,8},{12,10},{14,12},{16,14},{18,... | collective-permute-start | bytes 491528 | tf_op jit(solution)/shard_map/ppermute | solution.py:19
  76.0 7.5 %collective-permute-start.7 = (bf16[80,1024]{1,0:T(8,128)(2,1)S(1)}, bf16[80,1024]{1,0:T(8,128)(2,1)S(1)}, u32[]{:S(2)}, u32[]{:S(2)}) collective-permute-start(bf16[80,1024]{1,0:T(8,128)(2,1)S(1)} %collective-permute-done.6), channel_id=1, source_target_pairs={{0,2},{2,4},{4,6},{6,8},{8,10},{10,12},{12,14},{14,16},{16,18},{18... | collective-permute-start | bytes 491528 | tf_op jit(solution)/shard_map/ppermute | solution.py:18
  78.6 8.2 %collective-permute-start.14 = (bf16[80,1024]{1,0:T(8,128)(2,1)S(1)}, bf16[80,1024]{1,0:T(8,128)(2,1)S(1)}, u32[]{:S(2)}, u32[]{:S(2)}) collective-permute-start(bf16[80,1024]{1,0:T(8,128)(2,1)S(1)} %collective-permute-done.13), channel_id=1, source_target_pairs={{0,30},{2,0},{4,2},{6,4},{8,6},{10,8},{12,10},{14,12},{16,14},{18,... | collective-permute-start | bytes 491528 | tf_op jit(solution)/shard_map/ppermute | solution.py:19
  97.5 9.8 %all-to-all-start.1 = ((f32[16,1,80]{2,1,0:T(1,128)}), f32[16,1,80]{2,1,0:T(1,128)S(1)}, u32[]{:S(2)}, u32[]{:S(2)}) async-start(f32[16,1,80]{2,1,0:T(1,128)} %all_to_all.24), calls=%async_computation.1 | async-start | bytes 16384 | tf_op jit(solution)/shard_map/all_to_all | solution.py:99
